TPU v7x, 256 devices: a whole 4x4x8 slice. The times are simulated.
256 devices in a mesh: fsdp: 16 (over y, x), rep: 16 (over z, core).
Axes of the slice: x: 4, y: 4, z: 8, core: 2. Of those that a mesh axis runs over, the one named last changes fastest.
Arguments:
- gradient: float32 [11264, 8192], P('fsdp', 'rep'), may hold values from -6 to 6
- row_counts: int32 [16], replicated, may hold values from 1 to 704, 8192 in all
- owners: int32 [16, 16], P(None, 'rep'), may hold values from 0 to 15, as said below
- refresh_flags: int32 [16, 16], P(None, 'rep'), may hold values 0 or 1
- stat_left: float32 [16, 16, 512, 512], P('fsdp', 'rep'), as said below
- stat_right: float32 [16, 16, 512, 512], P('fsdp', 'rep'), as said below
- root_left: float32 [16, 16, 512, 512], P('fsdp', 'rep'), as said below
- root_right: float32 [16, 16, 512, 512], P('fsdp', 'rep'), as said below
Outputs:
- direction: bfloat16 [11264, 8192], P('fsdp')
- new_left: float32 [16, 16, 512, 512], P('fsdp', 'rep')
- new_right: float32 [16, 16, 512, 512], P('fsdp', 'rep')
Inputs may be any that keep to these rules, and one draw needn't show every extreme that they name: `owners`: in each column band of blocks every fsdp index owns exactly 1 block. `stat_left`: symmetric positive definite. `stat_right`: symmetric positive definite. `root_left`: symmetric positive definite. `root_right`: symmetric positive definite.
All inputs are finite; a program needn't handle non-finite values. No bound on the sum of `refresh_flags` on one device may be relied on, other than what follows from the above.
Results may differ from a plain program's by a relative error of at most 0.001.
Values may be sent and summed in bfloat16 or wider, within the bound.
No kernel may reach another device: no remote copies, remote signals or barrier semaphores. Data moves between devices by JAX's collectives and lax.ppermute only.
A program may use at most 128 MiB of HBM per device.

v0:
```python
import jax
import jax.numpy as jnp
from jax import lax
from jax.sharding import PartitionSpec as P

ITERS = 3
highest = lax.Precision.HIGHEST
stat_decay = 0.9
graft_eps = 1e-06


def matmul(left_part, right_part):
    return jnp.dot(left_part, right_part, precision=highest, preferred_element_type=jnp.float32)


def inverse_root(matrix, sweeps):
    identity = jnp.eye(matrix.shape[0], dtype=jnp.float32)
    scaling = 2.5 / jnp.sqrt(jnp.sum(matrix * matrix))
    current = identity * jnp.sqrt(jnp.sqrt(scaling))
    moment = matrix * scaling
    for sweep_pos in range(sweeps):
        factor = (5.0 * identity - moment) * 0.25
        current = matmul(current, factor)
        if sweep_pos + 1 < sweeps:
            squared = matmul(factor, factor)
            moment = matmul(matmul(squared, squared), moment)
    return current


def tile_update(grad_tile, left_stat, right_stat, old_left, old_right, refresh_now):
    fresh_left = stat_decay * left_stat + (1.0 - stat_decay) * matmul(grad_tile, grad_tile.T)
    fresh_right = stat_decay * right_stat + (1.0 - stat_decay) * matmul(grad_tile.T, grad_tile)
    left_root, right_root = lax.cond(
        refresh_now > 0,
        lambda: (inverse_root(fresh_left, ITERS), inverse_root(fresh_right, ITERS)),
        lambda: (old_left, old_right),
    )
    precond = matmul(matmul(left_root, grad_tile), right_root)
    graft_ratio = jnp.mean(grad_tile * grad_tile) / (jnp.mean(precond * precond) + graft_eps)
    return (fresh_left, fresh_right, (precond * jnp.sqrt(graft_ratio)).astype(jnp.bfloat16))


def slot_table(owners):
    band_count = owners.shape[0]
    same_owner = owners[:, None, :] == owners[None, :, :]
    ordinal = jnp.arange(band_count, dtype=jnp.int32)
    earlier = (ordinal[None, :] < ordinal[:, None])[:, :, None]
    return jnp.sum(jnp.where(same_owner & earlier, 1, 0), axis=1).astype(jnp.int32)


def flatten_blocks(values_in):
    return values_in.reshape((values_in.shape[0] * values_in.shape[1],) + values_in.shape[2:])


def update_items(block_items):
    return tile_update(*block_items)


def per_device(
    gradient, row_counts, owners, refresh_flags, stat_left, stat_right, root_left, root_right
):
    tile_size = stat_left.shape[-1]
    owner_index = lax.axis_index("fsdp")
    capacity, slab_width = gradient.shape
    band_count, columns = owners.shape
    slot_count = stat_left.shape[0]
    offsets = jnp.cumsum(row_counts) - row_counts
    slot_rank = slot_table(owners)
    holder = owners * slot_count + slot_rank
    band_ids = jnp.arange(band_count, dtype=jnp.int32)
    column_ids = jnp.arange(columns, dtype=jnp.int32)
    band_at = jnp.sum(
        jnp.where(holder[None, :, :] == band_ids[:, None, None], band_ids[None, :, None], 0), axis=1
    )
    my_bands = lax.dynamic_slice_in_dim(band_at, owner_index * slot_count, slot_count, 0)
    refresh_now = refresh_flags[my_bands, column_ids[None, :]]
    everything = lax.all_gather(gradient, "fsdp", axis=0, tiled=True)
    global_rows = my_bands[:, :, None] * tile_size + jnp.arange(tile_size, dtype=jnp.int32)
    source_index = jnp.sum((offsets <= global_rows[..., None]).astype(jnp.int32), axis=-1) - 1
    flat_index = source_index * capacity + global_rows - offsets[source_index]
    picked = jnp.take(everything, flat_index.reshape(-1), axis=0)
    picked = picked.reshape(slot_count, columns, tile_size, columns, tile_size)
    owned_tiles = picked[:, column_ids, :, column_ids, :].transpose(1, 0, 2, 3)
    fresh_lefts, fresh_rights, tile_stack = lax.map(
        update_items,
        (
            flatten_blocks(owned_tiles),
            flatten_blocks(stat_left),
            flatten_blocks(stat_right),
            flatten_blocks(root_left),
            flatten_blocks(root_right),
            refresh_now.reshape(-1),
        ),
    )
    new_left = fresh_lefts.reshape(stat_left.shape)
    new_right = fresh_rights.reshape(stat_right.shape)
    directions = tile_stack.reshape(slot_count, columns, tile_size, tile_size)
    gathered = lax.all_gather(directions, "fsdp", axis=0, tiled=True)
    local_rows = jnp.arange(capacity, dtype=jnp.int32)
    global_rows = offsets[owner_index] + local_rows
    live_rows = local_rows < row_counts[owner_index]
    band_pos = jnp.clip(global_rows // tile_size, 0, band_count - 1)
    within = global_rows % tile_size
    source_index = holder[band_pos]
    picked = gathered[source_index, column_ids[None, :], within[:, None]]
    row_slab = picked.reshape(capacity, slab_width)
    row_slab = jnp.where(live_rows[:, None], row_slab, jnp.zeros_like(row_slab))
    direction = lax.all_gather(row_slab, "rep", axis=1, tiled=True)
    return (direction, new_left, new_right)


def solution(mesh):
    return jax.shard_map(
        per_device,
        mesh=mesh,
        in_specs=(
            P("fsdp", "rep"),
            P(),
            P(None, "rep"),
            P(None, "rep"),
            P("fsdp", "rep", None, None),
            P("fsdp", "rep", None, None),
            P("fsdp", "rep", None, None),
            P("fsdp", "rep", None, None),
        ),
        out_specs=(P("fsdp", None), P("fsdp", "rep", None, None), P("fsdp", "rep", None, None)),
        check_vma=False,
    )
```

profile of v0, /device:TPU:1, one launch (start us, length us, event | category | flops | bytes accessed | tf_op | source)
XLA Modules:
  0.0 415.1 jit_solution(14211889260037414535)
XLA Ops:
  7.2 0.7 all-gather.5.cloned.1.call-update
  8.0 0.9 select_reduce_fusion.1
  12.9 1.3 fusion.111
  14.8 0.7 copy.17
  16.4 0.7 fusion.110
  17.2 4.3 %compare_select_fusion.13 = (s32[1,1,512,1]{2,3,1,0:T(1,128)S(1)}, s32[1,1,512,1]{2,3,1,0:T(1,128)S(1)}) fusion(s32[]{:T(128)} %bitcast.25, s32[]{:T(128)} %bitcast.26, s32[]{:T(128)} %bitcast.27, s32[]{:T(128)} %bitcast.28, s32[]{:T(128)} %bitcast.29, s32[]{:T(128)} %bitcast.31, s32[]{:T(128)} %bitcast.30, s32[1,1,512,1]{2,3,1,0:T(1,128)S(1)} %bitcast.118, ...), kind=kLoop, calls=%fused_computation.147 | loop fusion | flops 7168 | bytes 8220 | tf_op jit(solution)/shard_map/gather | solution.py:80
  21.6 5.7 %compare_and_fusion = (pred[512]{0:T(512)(128)(4,1)S(1)}, s32[512]{0:T(512)S(1)}) fusion(s32[]{:T(128)} %bitcast.13, s32[512]{0:T(512)S(1)} %convert_reduce_fusion, pred[512]{0:T(512)(128)(4,1)S(1)} %get-tuple-element.76, pred[512]{0:T(512)(128)(4,1)S(1)} %get-tuple-element.75, pred[512]{0:T(512)(128)(4,1)S(1)} %get-tuple-element.74, ...), kind=kLoop, calls=%fused_computation.173 | loop fusion | flops 10240 | bytes 11304 | tf_op jit(solution)/shard_map/jit(_take)/and | solution.py:81
  27.3 135.2 %all-gather.5.cloned.1.call-done = f32[11264,512]{1,0:T(8,128)} async-done(((f32[704,512]{1,0:T(8,128)}), f32[11264,512]{1,0:T(8,128)}) %all-gather.5.cloned.1.call-update) | async-done | bytes 23068688 | tf_op jit(solution)/shard_map/all_gather | solution.py:77
  162.5 9.6 %gather_fusion = f32[512,512]{1,0:T(8,128)S(1)} fusion(f32[11264,512]{1,0:T(8,128)} %all-gather.5.cloned.1.call-done, s32[1024]{0:T(1024)S(1)} %pad_clamp_fusion), kind=kCustom, calls=%fused_computation | custom fusion | bytes 2099200 | tf_op jit(solution)/shard_map/jit(_take)/gather | solution.py:81
  172.1 1.0 fusion.90
  173.1 4.4 %fusion.84 = f32[512,512]{1,0:T(8,128)} fusion(f32[1,1,512,512]{3,2,1,0:T(8,128)} %param.15, f32[512,512]{1,0:T(8,128)S(1)} %gather_fusion, pred[512]{0:T(512)(128)(4,1)S(1)} %get-tuple-element.77), kind=kOutput, calls=%fused_computation.88 | convolution fusion | flops 1611661312 | bytes 3146240 | tf_op jit(solution)/shard_map/while/body/eval_jaxpr/dot_general | solution.py:13
  177.5 4.2 %fusion.85 = f32[512,512]{1,0:T(8,128)} fusion(f32[1,1,512,512]{3,2,1,0:T(8,128)} %param.14, f32[512,512]{1,0:T(8,128)S(1)} %gather_fusion, pred[512]{0:T(512)(128)(4,1)S(1)} %get-tuple-element.77), kind=kOutput, calls=%fused_computation.90 | convolution fusion | flops 1611661312 | bytes 3146240 | tf_op jit(solution)/shard_map/while/body/eval_jaxpr/dot_general | solution.py:13
  181.8 47.2 %conditional.1 = (f32[512,512]{1,0:T(8,128)S(1)}, f32[512,512]{1,0:T(8,128)S(1)}) conditional(s32[]{:T(128)} %bitcast.10, (f32[1,1,512,512]{3,2,1,0:T(8,128)S(1)}, f32[1,1,512,512]{3,2,1,0:T(8,128)S(1)}) %tuple.88, (f32[512,512]{1,0:T(8,128)}, f32[512,512]{1,0:T(8,128)}) %tuple.20), branch_computations={%region_4.5_spmd, %region_5.8_spmd} | conditional | flops 29005185024 | bytes 48234624 | solution.py:33
  182.2 2.4 multiply_reduce_fusion
  186.1 3.1 fusion.6
  189.2 3.1 fusion.8
  192.3 3.6 fusion.22
  195.9 1.8 fusion.115
  197.7 3.1 fusion.10
  200.8 1.9 fusion.16
  202.7 2.3 fusion.14
  205.1 1.8 fusion.116
  206.9 1.8 fusion.1
  208.8 1.8 fusion.117
  210.6 3.6 fusion.25
  214.3 1.8 fusion.112
  216.1 3.1 fusion.12
  219.2 2.1 fusion.20
  221.3 1.9 fusion.18
  223.2 1.8 fusion.113
  225.1 1.9 fusion
  226.9 1.8 fusion.114
  229.0 3.0 fusion.86
  232.7 3.9 multiply_reduce_fusion.2
  237.4 0.9 multiply_convert_fusion
  238.9 0.7 compare_reduce_fusion.8
  239.6 0.7 compare_reduce_fusion.2
  240.3 0.7 compare_reduce_fusion.6
  241.0 0.7 compare_reduce_fusion.4
  241.7 0.7 compare_reduce_fusion
  242.4 0.7 fusion.109
  243.1 5.0 %fusion.98 = s32[704]{0:T(1024)S(1)} fusion(s32[]{:T(128)} %bitcast.51, s32[]{:T(128)} %bitcast.52, s32[]{:T(128)} %bitcast.53, s32[]{:T(128)} %bitcast.54, s32[]{:T(128)} %bitcast.55, s32[]{:T(128)} %bitcast.57, s32[]{:T(128)} %bitcast.56, s32[]{:T(128)} %bitcast.41), kind=kLoop, calls=%fused_computation.160 | loop fusion | flops 22528 | bytes 2848 | tf_op jit(solution)/shard_map/gather | solution.py:104
  249.3 5.6 %select_select_fusion = s32[704]{0:T(1024)S(1)} fusion(pred[704]{0:T(1024)(128)(4,1)S(1)} %get-tuple-element.121, pred[704]{0:T(1024)(128)(4,1)S(1)} %get-tuple-element.122, pred[704]{0:T(1024)(128)(4,1)S(1)} %get-tuple-element.123, pred[704]{0:T(1024)(128)(4,1)S(1)} %get-tuple-element.124, pred[704]{0:T(1024)(128)(4,1)S(1)} %get-tuple-element.125, ...), kind=kLoop, calls=%fused_computation.158 | loop fusion | flops 6336 | bytes 12004 | tf_op jit(solution)/shard_map/gather | solution.py:104
  255.0 59.0 %all-gather.9.cloned.1.call-done = bf16[8192,512]{1,0:T(8,128)(2,1)} async-done(((bf16[512,512]{1,0:T(8,128)(2,1)}), bf16[8192,512]{1,0:T(8,128)(2,1)}) %all-gather.9.cloned.1.call-update) | async-done | bytes 8388624 | tf_op jit(solution)/shard_map/all_gather | solution.py:98
  314.0 12.1 %gather_fusion.1 = bf16[704,512]{1,0:T(8,128)(2,1)S(1)} fusion(bf16[16,1,512,512]{3,2,1,0:T(8,128)(2,1)} %bitcast.114, s32[704]{0:T(1024)S(1)} %fusion.105), kind=kCustom, calls=%fused_computation.1 | custom fusion | bytes 1450240 | tf_op jit(solution)/shard_map/gather | solution.py:105
  326.1 1.0 broadcast_select_fusion
  327.2 71.1 %all-gather.7.cloned.1.call-done = bf16[704,8192]{1,0:T(8,128)(2,1)} async-done(((bf16[704,512]{1,0:T(8,128)(2,1)}), bf16[704,8192]{1,0:T(8,128)(2,1)}) %all-gather.7.cloned.1.call-update) | async-done | bytes 11534352 | tf_op jit(solution)/shard_map/all_gather | solution.py:108
  398.3 10.0 %copy.30 = bf16[704,8192]{1,0:T(8,128)(2,1)} copy(bf16[704,8192]{1,0:T(8,128)(2,1)} %all-gather.7.cloned.1.call-done) | data formatting | bytes 23068672
  (31 shorter events, 4.4 us)
Async XLA Ops:
  7.2 174.6 %copy-start = (f32[1,1,512,512]{3,2,1,0:T(8,128)S(1)}, f32[1,1,512,512]{3,2,1,0:T(8,128)}, u32[]{:S(2)}) copy-start(f32[1,1,512,512]{3,2,1,0:T(8,128)} %param.16) | copy-start | bytes 3145732
  7.2 174.6 %copy-start.1 = (f32[1,1,512,512]{3,2,1,0:T(8,128)S(1)}, f32[1,1,512,512]{3,2,1,0:T(8,128)}, u32[]{:S(2)}) copy-start(f32[1,1,512,512]{3,2,1,0:T(8,128)} %param.17) | copy-start | bytes 3145732
  7.2 155.3 %all-gather.5.cloned.1.call-start = ((), (), s32[]{:S(2)}) async-start(), calls=%async_computation | async-start | bytes 24510464 | tf_op jit(solution)/shard_map/all_gather | solution.py:77
  7.9 306.1 %all-gather.9.cloned.1.call-start = ((), (), s32[]{:S(2)}) async-start(), calls=%async_computation.2 | async-start | bytes 8912896 | tf_op jit(solution)/shard_map/all_gather | solution.py:98
  181.8 56.6 %copy-start.2 = (s32[16]{0:T(128)S(1)}, s32[16]{0:T(128)}, u32[]{:S(2)}) copy-start(s32[16]{0:T(128)} %param.11) | copy-start | bytes 196
  238.3 160.0 %all-gather.7.cloned.1.call-start = ((), (), s32[]{:S(2)}) async-start(), calls=%async_computation.1 | async-start | bytes 12255232 | tf_op jit(solution)/shard_map/all_gather | solution.py:108
Sparse Core Ops, SparseCore 0:
  10.4 152.0 all-gather.4
  238.4 75.5 all-gather.8
  327.3 70.9 all-gather.6
where the time goes:
time: 421 us; the launch traced here: 415 us
  waiting for transfers between devices  266 us (63%)
  matrix products  58.1 us (14%)
  local copies, waits for them, and re-layouts  35.1 us (8%)
  other arithmetic  34.8 us (8%)
  between operations  18.8 us (4%)
    all_gather x1, waiting for transfers between devices, per_device(): everything = lax.all_gather(gradient, 'fsdp', axis=0, tiled=True)  135 us
    all_gather x1, waiting for transfers between devices, per_device(): direction = lax.all_gather(row_slab, 'rep', axis=1, tiled=True)  71.1 us
    all_gather x1, waiting for transfers between devices, per_device(): gathered = lax.all_gather(directions, 'fsdp', axis=0, tiled=True)  59 us
    dot_general x22, matrix products, matmul(): jnp.dot(left_part, right_part, precision=highest, preferred_element_type=...  58.1 us
    gather x7, other arithmetic, per_device(): source_index = holder[band_pos]  14.1 us
    gather x1, local copies, waits for them, and re-layouts, per_device(): picked = gathered[source_index, column_ids[None, :], within[:, None]]  12.1 us
    unnamed x7, local copies, waits for them, and re-layouts  10 us
    gather x1, local copies, waits for them, and re-layouts, per_device(): picked = jnp.take(everything, flat_index.reshape(-1), axis=0)  9.59 us
  transfers between devices with their start and end apart: 3, of which 3 were waited for; matrix products, arithmetic and copies ran while one was open for 8% of the time, Pallas kernels for 0%

commit v1 on v0

--- a/solution.py
+++ b/solution.py
@@ -95,7 +95,8 @@
     new_left = fresh_lefts.reshape(stat_left.shape)
     new_right = fresh_rights.reshape(stat_right.shape)
     directions = tile_stack.reshape(slot_count, columns, tile_size, tile_size)
-    gathered = lax.all_gather(directions, "fsdp", axis=0, tiled=True)
+    sent = jnp.stack([directions] * lax.axis_size("fsdp"))
+    gathered = jnp.concatenate(lax.all_to_all(sent, "fsdp", 0, 0), axis=0)
     local_rows = jnp.arange(capacity, dtype=jnp.int32)
     global_rows = offsets[owner_index] + local_rows
     live_rows = local_rows < row_counts[owner_index]

time: 421 us -> 478 us (1.14)
  waiting for transfers between devices: 266 us -> 315 us
  starting transfers between devices: 0.12 us -> 5.17 us
    all_to_all x0 -> x1, waiting for transfers between devices: none -> 106 us  [per_device(): gathered = jnp.concatenate(lax.all_to_all(sent, 'fsdp', 0, 0), axis=0)]
    all_gather x1 -> x0, waiting for transfers between devices: 59 us -> none  [per_device(): gathered = lax.all_gather(directions, 'fsdp', axis=0, tiled=True)]
    all_to_all x0 -> x1, starting transfers between devices: none -> 5.09 us  [per_device(): gathered = jnp.concatenate(lax.all_to_all(sent, 'fsdp', 0, 0), axis=0)]
  transfers between devices with their start and end apart: 3 -> 3, of which waited for: 3 -> 3; matrix products, arithmetic and copies ran while one was open for 8% -> 7% of each run, Pallas kernels for 0% -> 0%
where the time goes in v1:
time: 478 us; the launch traced here: 473 us
  waiting for transfers between devices  315 us (66%)
  matrix products  58.1 us (12%)
  local copies, waits for them, and re-layouts  39.3 us (8%)
  other arithmetic  34 us (7%)
  between operations  19.2 us (4%)
  starting transfers between devices  5.17 us (1%)
    all_gather x1, waiting for transfers between devices, per_device(): everything = lax.all_gather(gradient, 'fsdp', axis=0, tiled=True)  135 us
    all_to_all x1, waiting for transfers between devices, per_device(): gathered = jnp.concatenate(lax.all_to_all(sent, 'fsdp', 0, 0), axis=0)  106 us
    all_gather x1, waiting for transfers between devices, per_device(): direction = lax.all_gather(row_slab, 'rep', axis=1, tiled=True)  72.9 us
    dot_general x22, matrix products, matmul(): jnp.dot(left_part, right_part, precision=highest, preferred_element_type=...  58.1 us
    gather x7, other arithmetic, per_device(): source_index = holder[band_pos]  14.1 us
    gather x1, local copies, waits for them, and re-layouts, per_device(): picked = gathered[source_index, column_ids[None, :], within[:, None]]  12.1 us
    unnamed x7, local copies, waits for them, and re-layouts  10 us
    gather x1, local copies, waits for them, and re-layouts, per_device(): picked = jnp.take(everything, flat_index.reshape(-1), axis=0)  9.59 us
  transfers between devices with their start and end apart: 3, of which 3 were waited for; matrix products, arithmetic and copies ran while one was open for 7% of the time, Pallas kernels for 0%

profile of v1, /device:TPU:1, one launch (start us, length us, event | category | flops | bytes accessed | tf_op | source)
XLA Modules:
  0.0 472.6 jit_solution(4706428350036857776)
XLA Ops:
  7.9 0.9 select_reduce_fusion.1
  12.9 1.3 fusion.111
  14.8 0.7 copy.16
  16.4 0.7 fusion.110
  17.2 4.3 compare_select_fusion.13
  21.6 5.7 %compare_and_fusion = (pred[512]{0:T(512)(128)(4,1)S(1)}, s32[512]{0:T(512)S(1)}) fusion(s32[]{:T(128)} %bitcast.13, s32[512]{0:T(512)S(1)} %convert_reduce_fusion, pred[512]{0:T(512)(128)(4,1)S(1)} %get-tuple-element.76, pred[512]{0:T(512)(128)(4,1)S(1)} %get-tuple-element.75, pred[512]{0:T(512)(128)(4,1)S(1)} %get-tuple-element.74, ...), kind=kLoop, calls=%fused_computation.173 | loop fusion | flops 10240 | bytes 11304 | tf_op jit(solution)/shard_map/jit(_take)/and | solution.py:81
  27.3 135.2 %all-gather.3.cloned.1.call-done = f32[11264,512]{1,0:T(8,128)} async-done(((f32[704,512]{1,0:T(8,128)}), f32[11264,512]{1,0:T(8,128)}) %all-gather.3.cloned.1.call-update) | async-done | bytes 23068688 | tf_op jit(solution)/shard_map/all_gather | solution.py:77
  162.5 9.6 %gather_fusion = f32[512,512]{1,0:T(8,128)S(1)} fusion(f32[11264,512]{1,0:T(8,128)} %all-gather.3.cloned.1.call-done, s32[1024]{0:T(1024)S(1)} %pad_clamp_fusion), kind=kCustom, calls=%fused_computation | custom fusion | bytes 2099200 | tf_op jit(solution)/shard_map/jit(_take)/gather | solution.py:81
  172.1 1.0 fusion.90
  173.1 4.4 fusion.84
  177.5 4.2 fusion.85
  181.8 46.8 %conditional.1 = (f32[512,512]{1,0:T(8,128)S(1)}, f32[512,512]{1,0:T(8,128)S(1)}) conditional(s32[]{:T(128)} %bitcast.10, (f32[1,1,512,512]{3,2,1,0:T(8,128)S(1)}, f32[1,1,512,512]{3,2,1,0:T(8,128)S(1)}) %tuple.86, (f32[512,512]{1,0:T(8,128)}, f32[512,512]{1,0:T(8,128)}) %tuple.20), branch_computations={%region_4.5_spmd, %region_5.8_spmd} | conditional | flops 29005185024 | bytes 48234624 | solution.py:33
  181.8 2.4 multiply_reduce_fusion
  185.6 3.1 fusion.6
  188.8 3.1 fusion.8
  191.9 3.6 fusion.22
  195.5 1.8 fusion.115
  197.3 3.1 fusion.10
  200.4 1.9 fusion.16
  202.3 2.3 fusion.14
  204.7 1.8 fusion.116
  206.5 1.9 fusion.1
  208.4 1.8 fusion.117
  210.2 3.6 fusion.25
  213.9 1.8 fusion.112
  215.7 3.1 fusion.12
  218.8 2.1 fusion.20
  220.9 1.9 fusion.18
  222.8 1.8 fusion.113
  224.7 1.9 fusion
  226.5 1.8 fusion.114
  228.6 3.0 fusion.86
  232.3 3.9 multiply_reduce_fusion.2
  237.1 4.2 stack.3
  241.3 5.1 %all-to-all-start = ((bf16[16,1,1,512,512]{4,3,2,1,0:T(8,128)(2,1)}), bf16[16,1,1,512,512]{4,3,2,1,0:T(8,128)(2,1)}, u32[]{:S(2)}, u32[]{:S(2)}) async-start(bf16[16,1,1,512,512]{4,3,2,1,0:T(8,128)(2,1)} %stack.3), calls=%async_computation | async-start | bytes 16777216 | tf_op jit(solution)/shard_map/all_to_all | solution.py:99
  247.0 0.7 compare_reduce_fusion.8
  247.7 0.7 compare_reduce_fusion.2
  248.4 0.7 compare_reduce_fusion.6
  249.1 0.7 compare_reduce_fusion.4
  249.8 0.7 compare_reduce_fusion
  250.5 0.7 fusion.109
  251.2 5.0 %fusion.98 = s32[704]{0:T(1024)S(1)} fusion(s32[]{:T(128)} %bitcast.50, s32[]{:T(128)} %bitcast.51, s32[]{:T(128)} %bitcast.52, s32[]{:T(128)} %bitcast.53, s32[]{:T(128)} %bitcast.54, s32[]{:T(128)} %bitcast.56, s32[]{:T(128)} %bitcast.55, s32[]{:T(128)} %bitcast.40), kind=kLoop, calls=%fused_computation.160 | loop fusion | flops 22528 | bytes 2848 | tf_op jit(solution)/shard_map/gather | solution.py:105
  257.5 5.6 %select_select_fusion = s32[704]{0:T(1024)S(1)} fusion(pred[704]{0:T(1024)(128)(4,1)S(1)} %get-tuple-element.121, pred[704]{0:T(1024)(128)(4,1)S(1)} %get-tuple-element.122, pred[704]{0:T(1024)(128)(4,1)S(1)} %get-tuple-element.123, pred[704]{0:T(1024)(128)(4,1)S(1)} %get-tuple-element.124, pred[704]{0:T(1024)(128)(4,1)S(1)} %get-tuple-element.125, ...), kind=kLoop, calls=%fused_computation.158 | loop fusion | flops 6336 | bytes 12004 | tf_op jit(solution)/shard_map/gather | solution.py:105
  263.1 106.3 %all-to-all-done = bf16[16,1,1,512,512]{4,3,2,1,0:T(8,128)(2,1)} async-done(((bf16[16,1,1,512,512]{4,3,2,1,0:T(8,128)(2,1)}), bf16[16,1,1,512,512]{4,3,2,1,0:T(8,128)(2,1)}, u32[]{:S(2)}, u32[]{:S(2)}) %all-to-all-start) | async-done | bytes 8388640 | tf_op jit(solution)/shard_map/all_to_all | solution.py:99
  369.5 12.1 %gather_fusion.1 = bf16[704,512]{1,0:T(8,128)(2,1)S(1)} fusion(bf16[16,1,512,512]{3,2,1,0:T(8,128)(2,1)} %bitcast.39, s32[704]{0:T(1024)S(1)} %fusion.105), kind=kCustom, calls=%fused_computation.1 | custom fusion | bytes 1450240 | tf_op jit(solution)/shard_map/gather | solution.py:106
  381.6 1.0 broadcast_select_fusion
  382.7 72.9 %all-gather.5.cloned.1.call-done = bf16[704,8192]{1,0:T(8,128)(2,1)} async-done(((bf16[704,512]{1,0:T(8,128)(2,1)}), bf16[704,8192]{1,0:T(8,128)(2,1)}) %all-gather.5.cloned.1.call-update) | async-done | bytes 11534352 | tf_op jit(solution)/shard_map/all_gather | solution.py:109
  455.5 10.0 %copy.28 = bf16[704,8192]{1,0:T(8,128)(2,1)} copy(bf16[704,8192]{1,0:T(8,128)(2,1)} %all-gather.5.cloned.1.call-done) | data formatting | bytes 23068672
  (31 shorter events, 5.2 us)
Async XLA Ops:
  7.2 174.6 %copy-start = (f32[1,1,512,512]{3,2,1,0:T(8,128)S(1)}, f32[1,1,512,512]{3,2,1,0:T(8,128)}, u32[]{:S(2)}) copy-start(f32[1,1,512,512]{3,2,1,0:T(8,128)} %param.16) | copy-start | bytes 3145732
  7.2 174.6 %copy-start.1 = (f32[1,1,512,512]{3,2,1,0:T(8,128)S(1)}, f32[1,1,512,512]{3,2,1,0:T(8,128)}, u32[]{:S(2)}) copy-start(f32[1,1,512,512]{3,2,1,0:T(8,128)} %param.17) | copy-start | bytes 3145732
  7.2 155.3 %all-gather.3.cloned.1.call-start = ((), (), s32[]{:S(2)}) async-start(), calls=%async_computation.1 | async-start | bytes 24510464 | tf_op jit(solution)/shard_map/all_gather | solution.py:77
  237.1 9.4 %copy-start.2 = (s32[16]{0:T(128)S(1)}, s32[16]{0:T(128)}, u32[]{:S(2)}) copy-start(s32[16]{0:T(128)} %param.11) | copy-start | bytes 196
  241.3 128.2 %all-to-all-start = ((bf16[16,1,1,512,512]{4,3,2,1,0:T(8,128)(2,1)}), bf16[16,1,1,512,512]{4,3,2,1,0:T(8,128)(2,1)}, u32[]{:S(2)}, u32[]{:S(2)}) async-start(bf16[16,1,1,512,512]{4,3,2,1,0:T(8,128)(2,1)} %stack.3), calls=%async_computation | async-start | bytes 16777216 | tf_op jit(solution)/shard_map/all_to_all | solution.py:99
  246.4 209.1 %all-gather.5.cloned.1.call-start = ((), (), s32[]{:S(2)}) async-start(), calls=%async_computation.2 | async-start | bytes 12255232 | tf_op jit(solution)/shard_map/all_gather | solution.py:109
Sparse Core Ops, SparseCore 0:
  10.4 151.9 all-gather.2
  382.8 72.6 all-gather.4
